TPU v7x, 512 devices: a whole 4x8x8 slice. The times are simulated.
512 devices in a mesh: seq: 64 (over x, y, z_hi), head: 8 (over z_lo, core).
Axes of the slice: x: 4, y: 8, z: 8 (z_hi: 2, z_lo: 4; z = z_hi * 4 + z_lo), core: 2. Of those that a mesh axis runs over, the one named last changes fastest.
Arguments:
- queries: bfloat16 [65536, 5120], P(('seq', 'head')), may hold values from -7.5 to 7.5
- keys: bfloat16 [65536, 1024], P(('seq', 'head')), may hold values from -7.5 to 7.5
- values: bfloat16 [65536, 1024], P(('seq', 'head')), may hold values from -6 to 6
- fetch_list: int32 [64, 64, 2], replicated, may hold values from 0 to 15, as said below
- choose: int32 [1024, 16], P('seq'), may hold values from 0 to 127, as said below
- live: int32 [1024], P('seq'), may hold values from 0 to 16, as said below
Outputs:
- attn_out: bfloat16 [65536, 5120], P(('seq', 'head'))
Inputs may be any that keep to these rules, and one draw needn't show every extreme that they name: Each row fetch_list[d, s] holds 2 distinct blocks. Each row of choose holds 16 distinct slots; slot j stands for entry j % 2 of fetch_list[d, j // 2]; the first live[b] entries of row b name slots j with j // 2 < b // 16. live[b] is at most 2 * (b // 16); every draw has a block with live equal to 16.
All inputs are finite; a program needn't handle non-finite values.
Results may differ from a plain program's by a relative error of at most 0.0042.
Values may be sent and summed in bfloat16 or wider, within the bound.
A program may use at most 64 MiB of HBM per device.

v0:
```python
import math

import jax
import jax.numpy as jnp
from jax import lax
from jax.sharding import PartitionSpec as P

HEAD_WIDTH = 128
BLOCK_TOKENS = 64
LISTED_ENTRIES = 16


def normalize(scores):
    highest = jnp.max(scores, axis=-1, keepdims=True)
    weights = jnp.exp(scores - highest)
    totals = jnp.sum(weights, axis=-1)
    return (weights.astype(jnp.bfloat16), totals)


def body(queries, keys, values, fetch_list, choose, live):
    scaling = 1.0 / math.sqrt(HEAD_WIDTH)
    q_all, k_all, v_all = (
        lax.all_to_all(queries, "head", split_axis=1, concat_axis=0, tiled=True),
        lax.all_to_all(keys, "head", split_axis=1, concat_axis=0, tiled=True),
        lax.all_to_all(values, "head", split_axis=1, concat_axis=0, tiled=True),
    )
    tokens_here = q_all.shape[0]
    kv_heads = k_all.shape[1] // HEAD_WIDTH
    q_heads = q_all.shape[1] // HEAD_WIDTH
    repeat_factor = q_heads // kv_heads
    blocks_here = tokens_here // BLOCK_TOKENS
    position = lax.axis_index("seq")
    wanted = lax.dynamic_index_in_dim(fetch_list, position, 1, keepdims=False)
    k_rows = k_all.reshape(blocks_here, BLOCK_TOKENS * kv_heads * HEAD_WIDTH)
    v_rows = v_all.reshape(blocks_here, BLOCK_TOKENS * kv_heads * HEAD_WIDTH)
    send_k = k_rows[wanted]
    send_v = v_rows[wanted]
    got_k, got_v = (
        lax.all_to_all(send_k, "seq", split_axis=0, concat_axis=0, tiled=True),
        lax.all_to_all(send_v, "seq", split_axis=0, concat_axis=0, tiled=True),
    )
    slot_count = got_k.shape[0] * got_k.shape[1]
    got_k = got_k.reshape(slot_count, BLOCK_TOKENS, kv_heads, HEAD_WIDTH)
    got_v = got_v.reshape(slot_count, BLOCK_TOKENS, kv_heads, HEAD_WIDTH)
    group_blocks = 1
    while group_blocks * BLOCK_TOKENS * q_heads < 512 and blocks_here % (2 * group_blocks) == 0:
        group_blocks = group_blocks * 2
    group_count = blocks_here // group_blocks
    q_groups = q_all.reshape(
        group_count, group_blocks, BLOCK_TOKENS, kv_heads, repeat_factor, HEAD_WIDTH
    )
    k_groups = k_all.reshape(group_count, group_blocks, BLOCK_TOKENS, kv_heads, HEAD_WIDTH)
    v_groups = v_all.reshape(group_count, group_blocks, BLOCK_TOKENS, kv_heads, HEAD_WIDTH)
    c_groups = choose.reshape(group_count, group_blocks, LISTED_ENTRIES)
    l_groups = live.reshape(group_count, group_blocks)

    def one_group(inputs):
        q_block, own_k, own_v, picked, counts = inputs
        imp_k = got_k[picked]
        imp_v = got_v[picked]
        keys_all = jnp.concatenate([own_k[:, None], imp_k], axis=1).reshape(
            group_blocks, (LISTED_ENTRIES + 1) * BLOCK_TOKENS, kv_heads, HEAD_WIDTH
        )
        vals_all = jnp.concatenate([own_v[:, None], imp_v], axis=1).reshape(
            group_blocks, (LISTED_ENTRIES + 1) * BLOCK_TOKENS, kv_heads, HEAD_WIDTH
        )
        scores = (
            jnp.einsum("bqhgd,bkhd->bhgqk", q_block, keys_all, preferred_element_type=jnp.float32)
            * scaling
        )
        column = jnp.arange((LISTED_ENTRIES + 1) * BLOCK_TOKENS, dtype=jnp.int32)
        query_row = jnp.arange(BLOCK_TOKENS, dtype=jnp.int32)
        key_block = column // BLOCK_TOKENS
        own_ok = ((key_block == 0)[None, :] & (column[None, :] <= query_row[:, None]))[None]
        import_ok = (key_block >= 1)[None, None, :] & (
            key_block[None, None, :] <= counts[:, None, None]
        )
        allowed = own_ok | import_ok
        scores = jnp.where(allowed[:, None, None], scores, -jnp.inf)
        rounded, totals = normalize(scores)
        mixed = jnp.einsum(
            "bhgqk,bkhd->bqhgd", rounded, vals_all, preferred_element_type=jnp.float32
        )
        result = mixed / jnp.transpose(totals, (0, 3, 1, 2))[..., None]
        return result.astype(jnp.bfloat16)

    outputs = lax.map(one_group, (q_groups, k_groups, v_groups, c_groups, l_groups))
    attended = outputs.reshape(tokens_here, q_heads * HEAD_WIDTH)
    return lax.all_to_all(attended, "head", split_axis=0, concat_axis=1, tiled=True)


def solution(mesh):
    placed = (
        P(("seq", "head"), None),
        P(("seq", "head"), None),
        P(("seq", "head"), None),
        P(),
        P("seq", None),
        P("seq"),
    )
    return jax.shard_map(
        body, mesh=mesh, in_specs=placed, out_specs=P(("seq", "head"), None), check_vma=False
    )
```

profile of v0, /device:TPU:6, one launch (start us, length us, event | category | flops | bytes accessed | tf_op | source)
XLA Modules:
  0.0 338.5 jit_solution(3984904693983250079)
XLA Ops:
  1.7 7.3 %all-to-all-start = ((bf16[128,8,128]{2,0,1:T(8,128)(2,1)}), bf16[128,8,128]{2,0,1:T(8,128)(2,1)S(1)}, u32[]{:S(2)}, u32[]{:S(2)}) async-start(bf16[128,8,128]{2,0,1:T(8,128)(2,1)} %copy_bitcast_fusion.2), calls=%async_computation | async-start | bytes 524288 | tf_op jit(solution)/shard_map/all_to_all | solution.py:25
  10.7 8.0 %all-to-all-done = bf16[128,8,128]{2,0,1:T(8,128)(2,1)S(1)} async-done(((bf16[128,8,128]{2,0,1:T(8,128)(2,1)}), bf16[128,8,128]{2,0,1:T(8,128)(2,1)S(1)}, u32[]{:S(2)}, u32[]{:S(2)}) %all-to-all-start) | async-done | bytes 262176 | tf_op jit(solution)/shard_map/all_to_all | solution.py:25
  18.7 4.0 %all-to-all-start.2 = ((bf16[128,8,128]{2,0,1:T(8,128)(2,1)}), bf16[128,8,128]{2,0,1:T(8,128)(2,1)}, u32[]{:S(2)}, u32[]{:S(2)}) async-start(bf16[128,8,128]{2,0,1:T(8,128)(2,1)} %copy_bitcast_fusion.1), calls=%async_computation.2 | async-start | bytes 524288 | tf_op jit(solution)/shard_map/all_to_all | solution.py:24
  23.9 8.5 %all-to-all-done.2 = bf16[128,8,128]{2,0,1:T(8,128)(2,1)} async-done(((bf16[128,8,128]{2,0,1:T(8,128)(2,1)}), bf16[128,8,128]{2,0,1:T(8,128)(2,1)}, u32[]{:S(2)}, u32[]{:S(2)}) %all-to-all-start.2) | async-done | bytes 262176 | tf_op jit(solution)/shard_map/all_to_all | solution.py:24
  32.4 4.3 %all-to-all-start.4 = ((bf16[128,8,640]{2,0,1:T(8,128)(2,1)}), bf16[128,8,640]{2,0,1:T(8,128)(2,1)}, u32[]{:S(2)}, u32[]{:S(2)}) async-start(bf16[128,8,640]{2,0,1:T(8,128)(2,1)} %bitcast.102), calls=%async_computation.4 | async-start | bytes 2621440 | tf_op jit(solution)/shard_map/all_to_all | solution.py:23
  39.2 2.6 reshape.311
  41.8 27.1 %all-to-all-done.4 = bf16[128,8,640]{2,0,1:T(8,128)(2,1)} async-done(((bf16[128,8,640]{2,0,1:T(8,128)(2,1)}), bf16[128,8,640]{2,0,1:T(8,128)(2,1)}, u32[]{:S(2)}, u32[]{:S(2)}) %all-to-all-start.4) | async-done | bytes 1310752 | tf_op jit(solution)/shard_map/all_to_all | solution.py:23
  68.9 16.7 %all-to-all-start.1 = ((bf16[64,2,8192]{2,1,0:T(2,128)(2,1)}), bf16[64,2,8192]{2,1,0:T(2,128)(2,1)}, u32[]{:S(2)}, u32[]{:S(2)}) async-start(bf16[64,2,8192]{2,1,0:T(2,128)(2,1)} %reshape.311), calls=%async_computation.1 | async-start | bytes 4194304 | tf_op jit(solution)/shard_map/all_to_all | solution.py:40
  88.6 2.6 reshape.319
  91.2 47.4 %all-to-all-done.1 = bf16[64,2,8192]{2,1,0:T(2,128)(2,1)} async-done(((bf16[64,2,8192]{2,1,0:T(2,128)(2,1)}), bf16[64,2,8192]{2,1,0:T(2,128)(2,1)}, u32[]{:S(2)}, u32[]{:S(2)}) %all-to-all-start.1) | async-done | bytes 2097184 | tf_op jit(solution)/shard_map/all_to_all | solution.py:40
  138.6 8.2 %all-to-all-start.3 = ((bf16[64,2,8192]{2,1,0:T(2,128)(2,1)}), bf16[64,2,8192]{2,1,0:T(2,128)(2,1)S(1)}, u32[]{:S(2)}, u32[]{:S(2)}) async-start(bf16[64,2,8192]{2,1,0:T(2,128)(2,1)} %reshape.319), calls=%async_computation.3 | async-start | bytes 4194304 | tf_op jit(solution)/shard_map/all_to_all | solution.py:39
  146.8 4.1 %reshape.289 = bf16[8,2,64,1,5,128]{5,4,2,1,0,3:T(8,128)(2,1)} reshape(bf16[8,128,640]{2,1,0:T(8,128)(2,1)} %bitcast.30) | data formatting | bytes 2621440 | tf_op jit(solution)/shard_map/reshape | solution.py:49
  150.9 3.0 copy.23
  154.0 4.5 %reshape.284 = bf16[128,64,1,128]{3,1,0,2:T(8,128)(2,1)} reshape(bf16[64,2,8192]{2,1,0:T(2,128)(2,1)} %all-to-all-done.1) | data formatting | bytes 4194304 | tf_op jit(solution)/shard_map/reshape | solution.py:44
  158.4 40.7 %all-to-all-done.3 = bf16[64,2,8192]{2,1,0:T(2,128)(2,1)S(1)} async-done(((bf16[64,2,8192]{2,1,0:T(2,128)(2,1)}), bf16[64,2,8192]{2,1,0:T(2,128)(2,1)S(1)}, u32[]{:S(2)}, u32[]{:S(2)}) %all-to-all-start.3) | async-done | bytes 2097184 | tf_op jit(solution)/shard_map/all_to_all | solution.py:39
  199.2 2.8 reshape.288
  202.0 93.8 %while.12 = (s32[]{:T(128)}, bf16[8,2,64,1,5,128]{5,2,4,1,3,0:T(8,128)(2,1)}, bf16[8,2,64,1,128]{4,2,1,3,0:T(8,128)(2,1)S(1)}, s32[8,2,16]{2,1,0:T(2,128)}, bf16...) while((s32[]{:T(128)}, ...), condition=%wide.region_3.4_spmd, body=%wide.region_0.3_spmd.sunk | while | flops 362421984 | bytes 14708233 | solution.py:87
  202.7 2.2 gather_fusion.1
  208.3 3.0 gather_fusion
  214.5 2.2 gather_fusion.1
  220.0 3.0 gather_fusion
  231.7 3.0 gather_fusion
  237.9 2.2 gather_fusion.1
  243.4 3.0 gather_fusion
  249.6 2.2 gather_fusion.1
  255.2 3.0 gather_fusion
  266.9 3.0 gather_fusion
  278.6 3.0 gather_fusion
  290.3 3.0 gather_fusion
  295.7 2.4 copy.24
  298.1 2.4 all_to_all.67
  300.5 35.7 %all_to_all.77 = bf16[8,128,640]{2,1,0:T(8,128)(2,1)S(1)} all-to-all(bf16[8,128,640]{2,1,0:T(8,128)(2,1)} %all_to_all.67), channel_id=1, replica_groups=mesh['seq'=64,'head'=8] {'head'}, dimensions={0} | all-to-all | bytes 2621440 | tf_op jit(solution)/shard_map/all_to_all | solution.py:89
  (157 shorter events, 72.6 us)
Async XLA Ops:
  0.0 1.0 copy-start
  0.0 22.7 %copy-start.1 = (bf16[128,5120]{1,0:T(8,128)(2,1)S(1)}, bf16[128,5120]{1,0:T(8,128)(2,1)}, u32[]{:S(2)}) copy-start(bf16[128,5120]{1,0:T(8,128)(2,1)} %param.8) | copy-start | bytes 3932164
  1.7 17.0 %all-to-all-start = ((bf16[128,8,128]{2,0,1:T(8,128)(2,1)}), bf16[128,8,128]{2,0,1:T(8,128)(2,1)S(1)}, u32[]{:S(2)}, u32[]{:S(2)}) async-start(bf16[128,8,128]{2,0,1:T(8,128)(2,1)} %copy_bitcast_fusion.2), calls=%async_computation | async-start | bytes 524288 | tf_op jit(solution)/shard_map/all_to_all | solution.py:25
  18.7 13.8 %all-to-all-start.2 = ((bf16[128,8,128]{2,0,1:T(8,128)(2,1)}), bf16[128,8,128]{2,0,1:T(8,128)(2,1)}, u32[]{:S(2)}, u32[]{:S(2)}) async-start(bf16[128,8,128]{2,0,1:T(8,128)(2,1)} %copy_bitcast_fusion.1), calls=%async_computation.2 | async-start | bytes 524288 | tf_op jit(solution)/shard_map/all_to_all | solution.py:24
  22.7 14.0 %copy-start.2 = (s32[64,64,2]{1,2,0:T(2,128)S(1)}, s32[64,64,2]{1,2,0:T(2,128)}, u32[]{:S(2)}) copy-start(s32[64,64,2]{1,2,0:T(2,128)} %param.11) | copy-start | bytes 98308
  32.4 36.5 %all-to-all-start.4 = ((bf16[128,8,640]{2,0,1:T(8,128)(2,1)}), bf16[128,8,640]{2,0,1:T(8,128)(2,1)}, u32[]{:S(2)}, u32[]{:S(2)}) async-start(bf16[128,8,640]{2,0,1:T(8,128)(2,1)} %bitcast.102), calls=%async_computation.4 | async-start | bytes 2621440 | tf_op jit(solution)/shard_map/all_to_all | solution.py:23
  68.9 69.7 %all-to-all-start.1 = ((bf16[64,2,8192]{2,1,0:T(2,128)(2,1)}), bf16[64,2,8192]{2,1,0:T(2,128)(2,1)}, u32[]{:S(2)}, u32[]{:S(2)}) async-start(bf16[64,2,8192]{2,1,0:T(2,128)(2,1)} %reshape.311), calls=%async_computation.1 | async-start | bytes 4194304 | tf_op jit(solution)/shard_map/all_to_all | solution.py:40
  91.2 55.5 %copy-start.3 = (s32[16]{0:T(128)S(1)}, s32[16]{0:T(128)}, u32[]{:S(2)}) copy-start(s32[16]{0:T(128)} %param.13) | copy-start | bytes 196
  138.6 60.6 %all-to-all-start.3 = ((bf16[64,2,8192]{2,1,0:T(2,128)(2,1)}), bf16[64,2,8192]{2,1,0:T(2,128)(2,1)S(1)}, u32[]{:S(2)}, u32[]{:S(2)}) async-start(bf16[64,2,8192]{2,1,0:T(2,128)(2,1)} %reshape.319), calls=%async_computation.3 | async-start | bytes 4194304 | tf_op jit(solution)/shard_map/all_to_all | solution.py:39
where the time goes:
time: 343 us; the launch traced here: 338 us
  waiting for transfers between devices  132 us (38%)
  local copies, waits for them, and re-layouts  85.6 us (25%)
  starting transfers between devices  40.5 us (12%)
  blocking collectives  35.7 us (10%)
  matrix products  23.6 us (7%)
  other arithmetic  20.8 us (6%)
    all_to_all x1, waiting for transfers between devices, body(): lax.all_to_all(send_v, 'seq', split_axis=0, concat_axis=0, tiled=True)  47.4 us
    all_to_all x1, waiting for transfers between devices, body(): lax.all_to_all(send_k, 'seq', split_axis=0, concat_axis=0, tiled=True)  40.7 us
    all_to_all x1, blocking collectives, body(): lax.all_to_all(attended, 'head', split_axis=0, concat_axis=1, tiled=True)  35.7 us
    all_to_all x1, waiting for transfers between devices, body(): lax.all_to_all(queries, 'head', split_axis=1, concat_axis=0, tiled=True)  27.1 us
    gather x8, local copies, waits for them, and re-layouts, one_group(): imp_v = got_v[picked]  24 us
    gather x8, local copies, waits for them, and re-layouts, one_group(): imp_k = got_k[picked]  17.9 us
    all_to_all x1, starting transfers between devices, body(): lax.all_to_all(send_v, 'seq', split_axis=0, concat_axis=0, tiled=True)  16.7 us
    dot_general x8, matrix products, one_group(): jnp.einsum('bqhgd,bkhd->bhgqk', q_block, keys_all, preferred_element_type...  13.1 us
  transfers between devices with their start and end apart: 5, of which 5 were waited for; matrix products, arithmetic and copies ran while one was open for 7% of the time, Pallas kernels for 0%

commit v1 on v0

v1 whole, which is shorter than its diff:
```python
import functools
import math

import jax
import jax.numpy as jnp
from jax import lax
from jax.experimental import pallas as pl
from jax.experimental.pallas import tpu as pltpu
from jax.sharding import PartitionSpec as P

MESH = pl.DeviceIdType.MESH
WIDTH = 128
BLOCK = 64
ENTRIES = 16
X, Y, Z = 4, 8, 2
PLANE = Y * Z
GROUP = 8
REPEAT = 5
ROWS = 128
TOKENS = GROUP * ROWS
BLOCKS = TOKENS // BLOCK
QW = REPEAT * WIDTH
SCALE = math.log2(math.e) / math.sqrt(WIDTH)


def mirrored(z, i):
    return i + z * (6 + 2 * lax.rem(i, 2) - 2 * i)


def xor3(a, b):
    out = 0
    for bit in (4, 2, 1):
        out = out + bit * lax.rem(lax.rem(a // bit, 2) + lax.rem(b // bit, 2), 2)
    return out


def place(g, t):
    return t if g == 0 or t in (0, Y // 2) else Y // 2 + t


def kernel(
    fetch, choose, live, q_in, k_in, v_in, o_out,
    q_all, out_buf, items_k, items_v, pick_k, pick_v, got_k, got_v,
    q_send, q_recv, k_send, k_recv, v_send, v_recv,
    z_send, z_recv, y_send, y_recv, x_send, x_recv, o_send, o_recv, local_sem,
):
    s = lax.axis_index("seq")
    i = lax.axis_index("head")
    x, y, z = s // PLANE, lax.rem(s // Z, Y), lax.rem(s, Z)
    h = mirrored(z, i)
    own_k, own_v = items_k[0], items_v[0]
    picks = (pick_k, pick_v)
    gots = (got_k, got_v)

    def seq_of(ax, ay, az):
        return (ax * Y + ay) * Z + az

    right = (seq_of(x, lax.rem(y + 1, Y), z), i)
    left = (seq_of(x, lax.rem(y + Y - 1, Y), z), i)
    across = (seq_of(x, y, 1 - z), mirrored(1 - z, h))

    barrier = pltpu.get_barrier_semaphore()
    for j in range(1, GROUP):
        pl.semaphore_signal(barrier, inc=1, device_id=(s, lax.rem(i + j, GROUP)), device_id_type=MESH)
    for peer in (right, left, across):
        pl.semaphore_signal(barrier, inc=1, device_id=peer, device_id_type=MESH)
    for j in range(1, X):
        pl.semaphore_signal(
            barrier, inc=1, device_id=(seq_of(lax.rem(x + j, X), y, z), i), device_id_type=MESH
        )

    for xo in range(1, X):
        @pl.when(xo > x)
        def _():
            for got in gots:
                got[pl.ds(xo * PLANE * 2, PLANE * 2)] = jnp.zeros((PLANE * 2, BLOCK, WIDTH), jnp.bfloat16)

    pl.semaphore_wait(barrier, GROUP - 1 + 3 + X - 1)

    def rows_of(p):
        return pl.ds(pl.multiple_of(p * ROWS, ROWS), ROWS)

    def head_copy(kv, p):
        src, send, recv = ((k_in, k_send, k_recv), (v_in, v_send, v_recv))[kv]
        col = pl.multiple_of(mirrored(z, p) * WIDTH, WIDTH)
        return pltpu.make_async_remote_copy(
            src_ref=src.at[:, :, pl.ds(col, WIDTH)],
            dst_ref=(own_k, own_v)[kv].at[pl.ds(2 * i, 2)],
            send_sem=send.at[p], recv_sem=recv.at[i],
            device_id=(s, p), device_id_type=MESH,
        )

    def head_arrival(kv, p):
        src, send, recv = ((k_in, k_send, k_recv), (v_in, v_send, v_recv))[kv]
        return pltpu.make_async_remote_copy(
            src_ref=src.at[:, :, pl.ds(0, WIDTH)],
            dst_ref=(own_k, own_v)[kv].at[pl.ds(2 * p, 2)],
            send_sem=send.at[p], recv_sem=recv.at[p],
            device_id=(s, p), device_id_type=MESH,
        )

    def q_copy(p):
        col = pl.multiple_of(mirrored(z, p) * QW, WIDTH)
        return pltpu.make_async_remote_copy(
            src_ref=q_in.at[:, pl.ds(col, QW)],
            dst_ref=q_all.at[rows_of(i), :],
            send_sem=q_send.at[p], recv_sem=q_recv.at[i],
            device_id=(s, p), device_id_type=MESH,
        )

    def q_arrival(p):
        return pltpu.make_async_remote_copy(
            src_ref=q_in.at[:, pl.ds(0, QW)],
            dst_ref=q_all.at[rows_of(p), :],
            send_sem=q_send.at[p], recv_sem=q_recv.at[p],
            device_id=(s, p), device_id_type=MESH,
        )

    own_col = pl.multiple_of(h * WIDTH, WIDTH)
    own = [
        pltpu.make_async_copy(k_in.at[:, :, pl.ds(own_col, WIDTH)], own_k.at[pl.ds(2 * i, 2)], local_sem.at[0]),
        pltpu.make_async_copy(v_in.at[:, :, pl.ds(own_col, WIDTH)], own_v.at[pl.ds(2 * i, 2)], local_sem.at[1]),
        pltpu.make_async_copy(
            q_in.at[:, pl.ds(pl.multiple_of(h * QW, WIDTH), QW)], q_all.at[rows_of(i), :], local_sem.at[2]
        ),
    ]
    for kv in range(2):
        for j in (4, 3, 5, 2, 6, 1, 7):
            head_copy(kv, lax.rem(i + j, GROUP)).start()
        own[kv].start()
    for j in (4, 3, 5, 2, 6, 1, 7):
        q_copy(lax.rem(i + j, GROUP)).start()
    own[2].start()

    def item(kv, g, t, other):
        return (items_k, items_v)[kv][other + 2 * place(g, t)]

    def ring_copy(g, t, other, kv):
        return pltpu.make_async_remote_copy(
            src_ref=item(kv, g, t, other), dst_ref=item(kv, g, t + 1, other),
            send_sem=y_send.at[g, t, other, kv], recv_sem=y_recv.at[g, t, other, kv],
            device_id=(right, left)[g], device_id_type=MESH,
        )

    def z_copy(kv):
        return pltpu.make_async_remote_copy(
            src_ref=item(kv, 0, 0, 0), dst_ref=item(kv, 0, 0, 1), send_sem=z_send.at[kv], recv_sem=z_recv.at[kv],
            device_id=across, device_id_type=MESH,
        )

    def x_copy(kv, dx, o):
        return pltpu.make_async_remote_copy(
            src_ref=picks[kv].at[dx - 1, pl.ds(o * 2, 2)],
            dst_ref=gots[kv].at[pl.ds((x * PLANE + o) * 2, 2)],
            send_sem=x_send.at[kv, dx - 1, o], recv_sem=x_recv.at[kv, x, o],
            device_id=(seq_of(lax.rem(x + dx, X), y, z), i), device_id_type=MESH,
        )

    def x_arrival(kv, xo, o):
        return pltpu.make_async_remote_copy(
            src_ref=picks[kv].at[0, pl.ds(o * 2, 2)],
            dst_ref=gots[kv].at[pl.ds((xo * PLANE + o) * 2, 2)],
            send_sem=x_send.at[kv, 0, o], recv_sem=x_recv.at[kv, xo, o],
            device_id=(seq_of(xo, y, z), i), device_id_type=MESH,
        )

    def select(kv, src, o):
        for e in range(2):
            at = fetch[(x * PLANE + o) * 2 + e]
            gots[kv][(x * PLANE + o) * 2 + e] = src[at]
        for dx in range(1, X):
            @pl.when(x + dx < X)
            def _():
                for e in range(2):
                    at = fetch[((x + dx) * PLANE + o) * 2 + e]
                    picks[kv][dx - 1, o * 2 + e] = src[at]

    def forward(kv, o):
        for dx in range(1, X):
            @pl.when(x + dx < X)
            def _():
                x_copy(kv, dx, o).start()

    pending = []

    def pick(kv, g, t, other):
        ay = lax.rem(y + (Y - t if g == 0 else t), Y)
        o = ay * Z + (1 - z if other else z)
        select(kv, item(kv, g, t, other), o)
        pending.append((kv, o))
        if len(pending) > 1:
            forward(*pending.pop(0))

    for kv in range(2):
        own[kv].wait()
        for j in range(1, GROUP):
            head_arrival(kv, lax.rem(i + j, GROUP)).wait_recv()
        ring_copy(0, 0, 0, kv).start()
        ring_copy(1, 0, 0, kv).start()
        z_copy(kv).start()
        pick(kv, 0, 0, 0)
    for kv in range(2):
        z_copy(kv).wait_recv()
        ring_copy(0, 0, 1, kv).start()
        ring_copy(1, 0, 1, kv).start()
        pick(kv, 0, 0, 1)
    half = Y // 2
    for t in range(1, half + 1):
        for other in range(2):
            for kv in range(2):
                for g in range(2):
                    if t == half and kv != g:
                        continue
                    ring_copy(g, t - 1, other, kv).wait_recv()
                    if t < half - 1 or (t == half - 1 and kv == g):
                        ring_copy(g, t, other, kv).start()
                    pick(kv, g, t, other)
    while pending:
        forward(*pending.pop(0))

    own[2].wait()
    for j in range(1, GROUP):
        q_arrival(lax.rem(i + j, GROUP)).wait_recv()
    for xo in range(X - 1):
        @pl.when(xo < x)
        def _():
            def one(o, carry):
                for kv in range(2):
                    x_arrival(kv, xo, o).wait_recv()
                return carry
            lax.fori_loop(0, PLANE, one, 0)

    def out_copy(p, half_block):
        return pltpu.make_async_remote_copy(
            src_ref=out_buf.at[pl.ds(pl.multiple_of((p * 2 + half_block) * BLOCK, BLOCK), BLOCK), :],
            dst_ref=o_out.at[pl.ds(half_block * BLOCK, BLOCK), pl.ds(pl.multiple_of(h * QW, WIDTH), QW)],
            send_sem=o_send.at[p, half_block], recv_sem=o_recv.at[i, half_block],
            device_id=(s, p), device_id_type=MESH,
        )

    def out_arrival(p, half_block):
        return pltpu.make_async_remote_copy(
            src_ref=out_buf.at[pl.ds(half_block * BLOCK, BLOCK), :],
            dst_ref=o_out.at[
                pl.ds(half_block * BLOCK, BLOCK), pl.ds(pl.multiple_of(mirrored(z, p) * QW, WIDTH), QW)
            ],
            send_sem=o_send.at[p, half_block], recv_sem=o_recv.at[p, half_block],
            device_id=(s, p), device_id_type=MESH,
        )

    contract_last = (((1,), (1,)), ((), ()))
    contract = (((1,), (0,)), ((), ()))

    def attend(b):
        first = pl.multiple_of(b * BLOCK, BLOCK)
        q_rows = q_all[pl.ds(first, BLOCK), :]
        q = jnp.concatenate([q_rows[:, g * WIDTH:(g + 1) * WIDTH] for g in range(REPEAT)], axis=0)
        slots = [choose[b, e] for e in range(ENTRIES)]
        k_listed = jnp.concatenate([got_k[slot] for slot in slots], axis=0)
        k_own = own_k[b]
        far = lax.dot_general(q, k_listed, contract_last, preferred_element_type=jnp.float32)
        near = lax.dot_general(q, k_own, contract_last, preferred_element_type=jnp.float32)
        column = lax.broadcasted_iota(jnp.int32, (1, ENTRIES * BLOCK), 1)
        far = jnp.where(column < live[b] * BLOCK, far, -jnp.inf)
        row = lax.rem(lax.broadcasted_iota(jnp.int32, (REPEAT * BLOCK, BLOCK), 0), BLOCK)
        near = jnp.where(lax.broadcasted_iota(jnp.int32, (REPEAT * BLOCK, BLOCK), 1) <= row, near, -jnp.inf)
        highest = jnp.maximum(jnp.max(far, axis=1, keepdims=True), jnp.max(near, axis=1, keepdims=True)) * SCALE
        far = jnp.exp2(far * SCALE - highest)
        near = jnp.exp2(near * SCALE - highest)
        totals = jnp.sum(far, axis=1, keepdims=True) + jnp.sum(near, axis=1, keepdims=True)
        v_listed = jnp.concatenate([got_v[slot] for slot in slots], axis=0)
        v_own = own_v[b]
        mixed = lax.dot_general(far.astype(jnp.bfloat16), v_listed, contract, preferred_element_type=jnp.float32)
        mixed += lax.dot_general(near.astype(jnp.bfloat16), v_own, contract, preferred_element_type=jnp.float32)
        result = (mixed / totals).astype(jnp.bfloat16)
        for g in range(REPEAT):
            out_buf[pl.ds(first, BLOCK), g * WIDTH:(g + 1) * WIDTH] = result[g * BLOCK:(g + 1) * BLOCK]

    def one_pair(t, carry):
        p = xor3(7 - i, t)
        attend(p * 2)

        @pl.when(t > 0)
        def _():
            out_copy(xor3(7 - i, t - 1), 1).start()

        attend(p * 2 + 1)

        @pl.when(t < GROUP - 1)
        def _():
            out_copy(p, 0).start()
        return carry

    lax.fori_loop(0, GROUP, one_pair, 0)
    back = pltpu.make_async_copy(
        out_buf.at[rows_of(i), :], o_out.at[:, pl.ds(pl.multiple_of(h * QW, WIDTH), QW)], local_sem.at[3]
    )
    back.start()

    for j in range(1, GROUP):
        p = lax.rem(i + j, GROUP)
        for kv in range(2):
            head_copy(kv, p).wait_send()
        q_copy(p).wait_send()
        for half_block in range(2):
            out_copy(p, half_block).wait_send()
    for kv in range(2):
        z_copy(kv).wait_send()
    for t in range(half):
        for other in range(2):
            for kv in range(2):
                for g in range(2):
                    if t < half - 1 or kv == g:
                        ring_copy(g, t, other, kv).wait_send()
    for dx in range(1, X):
        @pl.when(x + dx < X)
        def _():
            def one(o, carry):
                for kv in range(2):
                    x_copy(kv, dx, o).wait_send()
                return carry
            lax.fori_loop(0, PLANE, one, 0)
    back.wait()
    for j in range(1, GROUP):
        p = lax.rem(i + j, GROUP)
        for half_block in range(2):
            out_arrival(p, half_block).wait_recv()


def body(queries, keys, values, fetch_list, choose, live):
    s = lax.axis_index("seq")
    fetch = fetch_list.reshape(X, PLANE, X, PLANE, 2)
    fetch = lax.dynamic_index_in_dim(fetch, lax.rem(s, PLANE), 1, keepdims=False)
    fetch = lax.dynamic_index_in_dim(fetch, s // PLANE, 1, keepdims=False).reshape(-1)
    dma = pltpu.SemaphoreType.DMA
    half = Y // 2
    smem = pl.BlockSpec(memory_space=pltpu.SMEM)
    anywhere = pl.BlockSpec(memory_space=pl.ANY)
    bf16 = jnp.bfloat16
    return pl.pallas_call(
        kernel,
        out_shape=jax.ShapeDtypeStruct(queries.shape, bf16),
        in_specs=[smem, smem, smem, anywhere, anywhere, anywhere],
        out_specs=anywhere,
        scratch_shapes=[
            pltpu.VMEM((TOKENS, QW), bf16),
            pltpu.VMEM((TOKENS, QW), bf16),
            [pltpu.VMEM((BLOCKS, BLOCK, WIDTH), bf16)] * PLANE,
            [pltpu.VMEM((BLOCKS, BLOCK, WIDTH), bf16)] * PLANE,
            pltpu.VMEM((X - 1, PLANE * 2, BLOCK, WIDTH), bf16),
            pltpu.VMEM((X - 1, PLANE * 2, BLOCK, WIDTH), bf16),
            pltpu.VMEM((X * PLANE * 2, BLOCK, WIDTH), bf16),
            pltpu.VMEM((X * PLANE * 2, BLOCK, WIDTH), bf16),
            dma((GROUP,)), dma((GROUP,)), dma((GROUP,)), dma((GROUP,)), dma((GROUP,)), dma((GROUP,)),
            dma((2,)), dma((2,)),
            dma((2, half, 2, 2)), dma((2, half, 2, 2)),
            dma((2, X - 1, PLANE)), dma((2, X, PLANE)),
            dma((GROUP, 2)), dma((GROUP, 2)),
            dma((4,)),
        ],
        compiler_params=pltpu.CompilerParams(
            collective_id=0, has_side_effects=True, vmem_limit_bytes=56 * 1024 * 1024
        ),
    )(fetch, choose, live, queries, keys.reshape(-1, BLOCK, keys.shape[1]), values.reshape(-1, BLOCK, values.shape[1]))


def solution(mesh):
    placed = (
        P(("seq", "head"), None),
        P(("seq", "head"), None),
        P(("seq", "head"), None),
        P(),
        P("seq", None),
        P("seq"),
    )
    return jax.shard_map(
        body, mesh=mesh, in_specs=placed, out_specs=P(("seq", "head"), None), check_vma=False
    )
```

time: 343 us -> 159 us (0.46); the launches traced: 338 us -> 159 us
  Pallas kernels: 0 us -> 155 us
  waiting for transfers between devices: 132 us -> 0 us
  local copies, waits for them, and re-layouts: 85.6 us -> 4.25 us
  starting transfers between devices: 40.5 us -> 0 us
  blocking collectives: 35.7 us -> 0 us
  matrix products: 23.6 us -> 0 us
  other arithmetic: 20.8 us -> 0 us
    pallas_call x0 -> x1, Pallas kernels: none -> 155 us  [body(): pl.pallas_call(kernel, out_shape=jax.ShapeDtypeStruct(queries.shape, bf16...]
    all_to_all x5 -> x0, waiting for transfers between devices: 132 us -> none  [the longest x1 47.4 us: body(): lax.all_to_all(send_v, 'seq', split_axis=0, concat_axis=0, tiled=True)]
    gather x20 -> x0, local copies, waits for them, and re-layouts: 50.9 us -> none  [the longest x8 24 us: one_group(): imp_v = got_v[picked]]
    all_to_all x5 -> x0, starting transfers between devices: 40.5 us -> none  [the longest x1 16.7 us: body(): lax.all_to_all(send_v, 'seq', split_axis=0, concat_axis=0, tiled=True)]
    all_to_all x1 -> x0, blocking collectives: 35.7 us -> none  [body(): lax.all_to_all(attended, 'head', split_axis=0, concat_axis=1, tiled=True)]
    dot_general x16 -> x0, matrix products: 23.6 us -> none  [the longest x8 13.1 us: one_group(): jnp.einsum('bqhgd,bkhd->bhgqk', q_block, keys_all, preferred_element_type...]
    reshape x6 -> x2, local copies, waits for them, and re-layouts: 12.6 us -> 1.68 us  [the longest x1 1.03 us: body(): fetch = fetch_list.reshape(X, PLANE, X, PLANE, 2)]
    concatenate x16 -> x0, other arithmetic: 9.13 us -> none  [the longest x8 8.73 us: one_group(): jnp.concatenate([own_v[:, None], imp_v], axis=1)]
  transfers between devices with their start and end apart: 5 -> 0, of which waited for: 5 -> 0; matrix products, arithmetic and copies ran while one was open for 7% -> 0% of each run, Pallas kernels for 0% -> 0%
where the time goes in v1:
time: 159 us
  Pallas kernels  155 us (97%)
  local copies, waits for them, and re-layouts  4.25 us (3%)
    pallas_call x1, Pallas kernels, body(): pl.pallas_call(kernel, out_shape=jax.ShapeDtypeStruct(queries.shape, bf16...  155 us

profile of v1, /device:TPU:6, one launch (start us, length us, event | category | flops | bytes accessed | tf_op | source)
XLA Modules:
  0.0 159.1 jit_solution(5027163244512308040)
XLA Ops:
  0.0 1.0 reshape.15
  1.1 0.1 copy.9
  1.2 0.7 reshape.16.fetch
  1.8 154.9 %shard_map.64 = bf16[128,5120]{1,0:T(8,128)(2,1)} custom-call(s32[128]{0:T(128)} %reshape.16.fetch, s32[16,16]{1,0:T(8,128)} %choose.1, s32[16]{0:T(128)} %live.1, bf16[128,5120]{1,0:T(8,128)(2,1)} %q_in.1, bf16[2,64,1024]{2,1,0:T(8,128)(2,1)} %bitcast.8, bf16[2,64,1024]{2,1,0:T(8,128)(2,1)} %bitcast.9), custom_call_target="tpu_custom_call" | custom-call | tf_op jit(solution)/shard_map/pallas_call | solution.py:340
  156.7 2.5 %copy.11 = bf16[128,5120]{1,0:T(8,128)(2,1)} copy(bf16[128,5120]{1,0:T(8,128)(2,1)} %shard_map.64) | data formatting | bytes 2621440
  (1 shorter events, 0.0 us)

commit v2 on v1

--- a/solution.py
+++ b/solution.py
@@ -20,6 +20,7 @@
 TOKENS = GROUP * ROWS
 BLOCKS = TOKENS // BLOCK
 QW = REPEAT * WIDTH
+LAG = 4
 SCALE = math.log2(math.e) / math.sqrt(WIDTH)
 
 
@@ -40,16 +41,15 @@
 
 def kernel(
     fetch, choose, live, q_in, k_in, v_in, o_out,
-    q_all, out_buf, items_k, items_v, pick_k, pick_v, got_k, got_v,
+    q_all, out_buf, items_k, items_v, pick_k, pick_v, relay_k, relay_v, got_k, got_v,
     q_send, q_recv, k_send, k_recv, v_send, v_recv,
-    z_send, z_recv, y_send, y_recv, x_send, x_recv, o_send, o_recv, local_sem,
+    z_send, z_recv, y_send, y_recv, x_send, x_recv, w_send, w_recv, r_send, r_recv, o_send, o_recv, local_sem,
 ):
     s = lax.axis_index("seq")
     i = lax.axis_index("head")
     x, y, z = s // PLANE, lax.rem(s // Z, Y), lax.rem(s, Z)
     h = mirrored(z, i)
     own_k, own_v = items_k[0], items_v[0]
-    picks = (pick_k, pick_v)
     gots = (got_k, got_v)
 
     def seq_of(ax, ay, az):
@@ -57,7 +57,8 @@
 
     right = (seq_of(x, lax.rem(y + 1, Y), z), i)
     left = (seq_of(x, lax.rem(y + Y - 1, Y), z), i)
-    across = (seq_of(x, y, 1 - z), mirrored(1 - z, h))
+    twin = mirrored(1 - z, h)
+    across = (seq_of(x, y, 1 - z), twin)
 
     barrier = pltpu.get_barrier_semaphore()
     for j in range(1, GROUP):
@@ -65,9 +66,10 @@
     for peer in (right, left, across):
         pl.semaphore_signal(barrier, inc=1, device_id=peer, device_id_type=MESH)
     for j in range(1, X):
-        pl.semaphore_signal(
-            barrier, inc=1, device_id=(seq_of(lax.rem(x + j, X), y, z), i), device_id_type=MESH
-        )
+        for az, ai in ((z, i), (1 - z, twin)):
+            pl.semaphore_signal(
+                barrier, inc=1, device_id=(seq_of(lax.rem(x + j, X), y, az), ai), device_id_type=MESH
+            )
 
     for xo in range(1, X):
         @pl.when(xo > x)
@@ -75,7 +77,7 @@
             for got in gots:
                 got[pl.ds(xo * PLANE * 2, PLANE * 2)] = jnp.zeros((PLANE * 2, BLOCK, WIDTH), jnp.bfloat16)
 
-    pl.semaphore_wait(barrier, GROUP - 1 + 3 + X - 1)
+    pl.semaphore_wait(barrier, GROUP - 1 + 3 + 2 * (X - 1))
 
     def rows_of(p):
         return pl.ds(pl.multiple_of(p * ROWS, ROWS), ROWS)
@@ -133,7 +135,7 @@
     own[2].start()
 
     def item(kv, g, t, other):
-        return (items_k, items_v)[kv][other + 2 * place(g, t)]
+        return items_v[place(g, t)] if kv else items_k[other + 2 * place(g, t)]
 
     def ring_copy(g, t, other, kv):
         return pltpu.make_async_remote_copy(
@@ -148,48 +150,119 @@
             device_id=across, device_id_type=MESH,
         )
 
-    def x_copy(kv, dx, o):
-        return pltpu.make_async_remote_copy(
-            src_ref=picks[kv].at[dx - 1, pl.ds(o * 2, 2)],
-            dst_ref=gots[kv].at[pl.ds((x * PLANE + o) * 2, 2)],
-            send_sem=x_send.at[kv, dx - 1, o], recv_sem=x_recv.at[kv, x, o],
+    def wanted(ax, az, o, e):
+        return fetch[((ax * Z + az) * PLANE + o) * 2 + e]
+
+    def x_copy(dx, o):
+        return pltpu.make_async_remote_copy(
+            src_ref=pick_k.at[dx - 1, pl.ds(o * 2, 2)],
+            dst_ref=got_k.at[pl.ds((x * PLANE + o) * 2, 2)],
+            send_sem=x_send.at[dx - 1, o], recv_sem=x_recv.at[x, o],
             device_id=(seq_of(lax.rem(x + dx, X), y, z), i), device_id_type=MESH,
         )
 
-    def x_arrival(kv, xo, o):
-        return pltpu.make_async_remote_copy(
-            src_ref=picks[kv].at[0, pl.ds(o * 2, 2)],
-            dst_ref=gots[kv].at[pl.ds((xo * PLANE + o) * 2, 2)],
-            send_sem=x_send.at[kv, 0, o], recv_sem=x_recv.at[kv, xo, o],
+    def x_arrival(xo, o):
+        return pltpu.make_async_remote_copy(
+            src_ref=pick_k.at[0, pl.ds(o * 2, 2)],
+            dst_ref=got_k.at[pl.ds((xo * PLANE + o) * 2, 2)],
+            send_sem=x_send.at[0, o], recv_sem=x_recv.at[xo, o],
             device_id=(seq_of(xo, y, z), i), device_id_type=MESH,
         )
 
-    def select(kv, src, o):
+    def w_copy(dx, dz, oy):
+        return pltpu.make_async_remote_copy(
+            src_ref=pick_v.at[dx * Z + dz, pl.ds(oy * 2, 2)],
+            dst_ref=got_v.at[pl.ds((x * PLANE + oy * Z + z) * 2, 2)],
+            send_sem=w_send.at[dx * Z + dz, oy], recv_sem=w_recv.at[x, oy * Z + z],
+            device_id=(seq_of(lax.rem(x + dx, X), y, 1 - z if dz else z), twin if dz else i), device_id_type=MESH,
+        )
+
+    def w_arrival(xo, o):
+        return pltpu.make_async_remote_copy(
+            src_ref=pick_v.at[0, pl.ds(0, 2)],
+            dst_ref=got_v.at[pl.ds((xo * PLANE + o) * 2, 2)],
+            send_sem=w_send.at[0, 0], recv_sem=w_recv.at[xo, o],
+            device_id=across, device_id_type=MESH,
+        )
+
+    def relay_parts(kv, oy, o):
+        if kv == 0:
+            yield pick_k.at[1, pl.ds(o * 2, 2)], x_send.at[1, o], relay_k.at[pl.ds(o * 2, 2)], o, (
+                got_k.at[pl.ds(o * 2, 2)], x_recv.at[0, o], (seq_of(2, y, z), i))
+        else:
+            for dz in range(2):
+                yield pick_v.at[2 * Z + dz, pl.ds(oy * 2, 2)], w_send.at[2 * Z + dz, oy], relay_v.at[dz, pl.ds(oy * 2, 2)], (
+                    PLANE + dz * Y + oy), (
+                    got_v.at[pl.ds((oy * Z + z) * 2, 2)], w_recv.at[0, oy * Z + z],
+                    (seq_of(2, y, 1 - z if dz else z), twin if dz else i))
+
+    def relay_in(kv, oy, o):
+        return [
+            pltpu.make_async_remote_copy(
+                src_ref=src, dst_ref=buf, send_sem=send, recv_sem=r_recv.at[n],
+                device_id=(seq_of(X - 1, y, z), i), device_id_type=MESH,
+            )
+            for src, send, buf, n, _ in relay_parts(kv, oy, o)
+        ]
+
+    def relay_out(kv, oy, o):
+        return [
+            pltpu.make_async_remote_copy(
+                src_ref=buf, dst_ref=to[0], send_sem=r_send.at[n], recv_sem=to[1],
+                device_id=to[2], device_id_type=MESH,
+            )
+            for _, _, buf, n, to in relay_parts(kv, oy, o)
+        ]
+
+    def select(kv, src, oy, o):
         for e in range(2):
-            at = fetch[(x * PLANE + o) * 2 + e]
-            gots[kv][(x * PLANE + o) * 2 + e] = src[at]
-        for dx in range(1, X):
+            gots[kv][(x * PLANE + o) * 2 + e] = src[wanted(x, z, o, e)]
+        for dx in range(X):
             @pl.when(x + dx < X)
             def _():
                 for e in range(2):
-                    at = fetch[((x + dx) * PLANE + o) * 2 + e]
-                    picks[kv][dx - 1, o * 2 + e] = src[at]
-
-    def forward(kv, o):
-        for dx in range(1, X):
-            @pl.when(x + dx < X)
-            def _():
-                x_copy(kv, dx, o).start()
+                    if kv == 0 and dx > 0:
+                        pick_k[dx - 1, o * 2 + e] = src[wanted(x + dx, z, o, e)]
+                    if kv == 1:
+                        pick_v[dx * Z + 1, oy * 2 + e] = src[wanted(x + dx, 1 - z, o, e)]
+                        if dx > 0:
+                            pick_v[dx * Z, oy * 2 + e] = src[wanted(x + dx, z, o, e)]
+
+    def forward(kv, oy, o):
+        for dx in range(X - 1, -1, -1):
+            def direct():
+                if kv == 1:
+                    w_copy(dx, 1, oy).start()
+                if dx > 0:
+                    (x_copy(dx, o) if kv == 0 else w_copy(dx, 0, oy)).start()
+            if dx == 2:
+                @pl.when(x == 0)
+                def _():
+                    for copy in relay_in(kv, oy, o):
+                        copy.start()
+                pl.when(x == 1)(direct)
+            else:
+                pl.when(x + dx < X)(direct)
+
+    def relay(kv, oy, o):
+        @pl.when(x == X - 1)
+        def _():
+            for copy in relay_in(kv, oy, o):
+                copy.wait_recv()
+            for copy in relay_out(kv, oy, o):
+                copy.start()
 
     pending = []
 
     def pick(kv, g, t, other):
-        ay = lax.rem(y + (Y - t if g == 0 else t), Y)
-        o = ay * Z + (1 - z if other else z)
-        select(kv, item(kv, g, t, other), o)
-        pending.append((kv, o))
+        oy = lax.rem(y + (Y - t if g == 0 else t), Y)
+        o = oy * Z + (1 - z if other else z)
+        select(kv, item(kv, g, t, other), oy, o)
+        pending.append((kv, oy, o))
         if len(pending) > 1:
-            forward(*pending.pop(0))
+            forward(*pending[-2])
+        if len(pending) > LAG:
+            relay(*pending[-LAG - 1])
 
     for kv in range(2):
         own[kv].wait()
@@ -197,38 +270,41 @@
             head_arrival(kv, lax.rem(i + j, GROUP)).wait_recv()
         ring_copy(0, 0, 0, kv).start()
         ring_copy(1, 0, 0, kv).start()
-        z_copy(kv).start()
+        if kv == 0:
+            z_copy(0).start()
         pick(kv, 0, 0, 0)
-    for kv in range(2):
-        z_copy(kv).wait_recv()
-        ring_copy(0, 0, 1, kv).start()
-        ring_copy(1, 0, 1, kv).start()
-        pick(kv, 0, 0, 1)
+    z_copy(0).wait_recv()
+    ring_copy(0, 0, 1, 0).start()
+    ring_copy(1, 0, 1, 0).start()
+    pick(0, 0, 0, 1)
     half = Y // 2
+    travels = ((1, 0), (0, 0), (0, 1))
     for t in range(1, half + 1):
-        for other in range(2):
-            for kv in range(2):
-                for g in range(2):
-                    if t == half and kv != g:
-                        continue
-                    ring_copy(g, t - 1, other, kv).wait_recv()
-                    if t < half - 1 or (t == half - 1 and kv == g):
-                        ring_copy(g, t, other, kv).start()
-                    pick(kv, g, t, other)
-    while pending:
-        forward(*pending.pop(0))
+        for kv, other in travels:
+            for g in range(2):
+                if t == half and g != (kv + other) % 2:
+                    continue
+                ring_copy(g, t - 1, other, kv).wait_recv()
+                if t < half - 1 or (t == half - 1 and g == (kv + other) % 2):
+                    ring_copy(g, t, other, kv).start()
+                pick(kv, g, t, other)
+    forward(*pending[-1])
+    for step in pending[-LAG:]:
+        relay(*step)
 
     own[2].wait()
     for j in range(1, GROUP):
         q_arrival(lax.rem(i + j, GROUP)).wait_recv()
-    for xo in range(X - 1):
+    for xo in range(X):
         @pl.when(xo < x)
         def _():
             def one(o, carry):
-                for kv in range(2):
-                    x_arrival(kv, xo, o).wait_recv()
+                x_arrival(xo, o).wait_recv()
+                w_arrival(xo, o).wait_recv()
                 return carry
             lax.fori_loop(0, PLANE, one, 0)
+    for oy in range(Y):
+        w_arrival(x, oy * Z + 1 - z).wait_recv()
 
     def out_copy(p, half_block):
         return pltpu.make_async_remote_copy(
@@ -304,22 +380,31 @@
         q_copy(p).wait_send()
         for half_block in range(2):
             out_copy(p, half_block).wait_send()
-    for kv in range(2):
-        z_copy(kv).wait_send()
+    z_copy(0).wait_send()
     for t in range(half):
-        for other in range(2):
-            for kv in range(2):
-                for g in range(2):
-                    if t < half - 1 or kv == g:
-                        ring_copy(g, t, other, kv).wait_send()
-    for dx in range(1, X):
+        for kv, other in travels:
+            for g in range(2):
+                if t < half - 1 or g == (kv + other) % 2:
+                    ring_copy(g, t, other, kv).wait_send()
+    for dx in range(X):
         @pl.when(x + dx < X)
         def _():
-            def one(o, carry):
-                for kv in range(2):
-                    x_copy(kv, dx, o).wait_send()
+            def one(oy, carry):
+                w_copy(dx, 1, oy).wait_send()
+                if dx > 0:
+                    w_copy(dx, 0, oy).wait_send()
+                    x_copy(dx, oy * Z).wait_send()
+                    x_copy(dx, oy * Z + 1).wait_send()
                 return carry
-            lax.fori_loop(0, PLANE, one, 0)
+            lax.fori_loop(0, Y, one, 0)
+    @pl.when(x == X - 1)
+    def _():
+        def one(oy, carry):
+            for kv, az in ((0, 0), (0, 1), (1, z)):
+                for copy in relay_out(kv, oy, oy * Z + az):
+                    copy.wait_send()
+            return carry
+        lax.fori_loop(0, Y, one, 0)
     back.wait()
     for j in range(1, GROUP):
         p = lax.rem(i + j, GROUP)
@@ -329,9 +414,9 @@
 
 def body(queries, keys, values, fetch_list, choose, live):
     s = lax.axis_index("seq")
-    fetch = fetch_list.reshape(X, PLANE, X, PLANE, 2)
-    fetch = lax.dynamic_index_in_dim(fetch, lax.rem(s, PLANE), 1, keepdims=False)
-    fetch = lax.dynamic_index_in_dim(fetch, s // PLANE, 1, keepdims=False).reshape(-1)
+    fetch = fetch_list.reshape(X, Y, Z, X, PLANE, 2)
+    fetch = lax.dynamic_index_in_dim(fetch, lax.rem(s // Z, Y), 1, keepdims=False)
+    fetch = lax.dynamic_index_in_dim(fetch, s // PLANE, 2, keepdims=False).reshape(-1)
     dma = pltpu.SemaphoreType.DMA
     half = Y // 2
     smem = pl.BlockSpec(memory_space=pltpu.SMEM)
@@ -346,15 +431,19 @@
             pltpu.VMEM((TOKENS, QW), bf16),
             pltpu.VMEM((TOKENS, QW), bf16),
             [pltpu.VMEM((BLOCKS, BLOCK, WIDTH), bf16)] * PLANE,
-            [pltpu.VMEM((BLOCKS, BLOCK, WIDTH), bf16)] * PLANE,
+            [pltpu.VMEM((BLOCKS, BLOCK, WIDTH), bf16)] * Y,
             pltpu.VMEM((X - 1, PLANE * 2, BLOCK, WIDTH), bf16),
-            pltpu.VMEM((X - 1, PLANE * 2, BLOCK, WIDTH), bf16),
+            pltpu.VMEM((X * Z, Y * 2, BLOCK, WIDTH), bf16),
+            pltpu.VMEM((PLANE * 2, BLOCK, WIDTH), bf16),
+            pltpu.VMEM((Z, Y * 2, BLOCK, WIDTH), bf16),
             pltpu.VMEM((X * PLANE * 2, BLOCK, WIDTH), bf16),
             pltpu.VMEM((X * PLANE * 2, BLOCK, WIDTH), bf16),
             dma((GROUP,)), dma((GROUP,)), dma((GROUP,)), dma((GROUP,)), dma((GROUP,)), dma((GROUP,)),
-            dma((2,)), dma((2,)),
+            dma((1,)), dma((1,)),
             dma((2, half, 2, 2)), dma((2, half, 2, 2)),
-            dma((2, X - 1, PLANE)), dma((2, X, PLANE)),
+            dma((X - 1, PLANE)), dma((X, PLANE)),
+            dma((X * Z, Y)), dma((X, PLANE)),
+            dma((2 * PLANE,)), dma((2 * PLANE,)),
             dma((GROUP, 2)), dma((GROUP, 2)),
             dma((4,)),
         ],

time: 159 us -> 155 us (0.975); the launches traced: 159 us -> 153 us
  Pallas kernels: 155 us -> 149 us
    pallas_call x1, Pallas kernels: 155 us -> 149 us  [body(): pl.pallas_call(kernel, out_shape=jax.ShapeDtypeStruct(queries.shape, bf16...]
where the time goes in v2:
time: 155 us; the launch traced here: 153 us
  Pallas kernels  149 us (96%)
  local copies, waits for them, and re-layouts  4.33 us (3%)
    pallas_call x1, Pallas kernels, body(): pl.pallas_call(kernel, out_shape=jax.ShapeDtypeStruct(queries.shape, bf16...  149 us

profile of v2, /device:TPU:6, one launch (start us, length us, event | category | flops | bytes accessed | tf_op | source)
XLA Modules:
  0.0 153.4 jit_solution(15387257766966496140)
XLA Ops:
  0.0 1.0 reshape.15
  1.1 0.1 copy.8
  1.2 0.7 reshape.16.fetch
  1.9 149.0 %shard_map.64 = bf16[128,5120]{1,0:T(8,128)(2,1)} custom-call(s32[256]{0:T(256)} %reshape.16.fetch, s32[16,16]{1,0:T(8,128)} %choose.1, s32[16]{0:T(128)} %live.1, bf16[128,5120]{1,0:T(8,128)(2,1)} %q_in.1, bf16[2,64,1024]{2,1,0:T(8,128)(2,1)} %bitcast.8, bf16[2,64,1024]{2,1,0:T(8,128)(2,1)} %bitcast.9), custom_call_target="tpu_custom_call" | custom-call | tf_op jit(solution)/shard_map/pallas_call | solution.py:425
  150.9 2.5 %copy.10 = bf16[128,5120]{1,0:T(8,128)(2,1)} copy(bf16[128,5120]{1,0:T(8,128)(2,1)} %shard_map.64) | data formatting | bytes 2621440
  (1 shorter events, 0.0 us)

commit v3 on v2

--- a/solution.py
+++ b/solution.py
@@ -20,7 +20,7 @@
 TOKENS = GROUP * ROWS
 BLOCKS = TOKENS // BLOCK
 QW = REPEAT * WIDTH
-LAG = 4
+Q_FIRST, Q_EVERY = 3, 2
 SCALE = math.log2(math.e) / math.sqrt(WIDTH)
 
 
@@ -41,9 +41,9 @@
 
 def kernel(
     fetch, choose, live, q_in, k_in, v_in, o_out,
-    q_all, out_buf, items_k, items_v, pick_k, pick_v, relay_k, relay_v, got_k, got_v,
+    q_all, out_buf, items_k, items_v, pick_k, pick_v, got_k, got_v,
     q_send, q_recv, k_send, k_recv, v_send, v_recv,
-    z_send, z_recv, y_send, y_recv, x_send, x_recv, w_send, w_recv, r_send, r_recv, o_send, o_recv, local_sem,
+    z_send, z_recv, y_send, y_recv, x_send, x_recv, w_send, w_recv, o_send, o_recv, local_sem,
 ):
     s = lax.axis_index("seq")
     i = lax.axis_index("head")
@@ -130,16 +130,18 @@
         for j in (4, 3, 5, 2, 6, 1, 7):
             head_copy(kv, lax.rem(i + j, GROUP)).start()
         own[kv].start()
-    for j in (4, 3, 5, 2, 6, 1, 7):
-        q_copy(lax.rem(i + j, GROUP)).start()
     own[2].start()
 
     def item(kv, g, t, other):
         return items_v[place(g, t)] if kv else items_k[other + 2 * place(g, t)]
 
     def ring_copy(g, t, other, kv):
-        return pltpu.make_async_remote_copy(
-            src_ref=item(kv, g, t, other), dst_ref=item(kv, g, t + 1, other),
+        src, dst = item(kv, g, t, other), item(kv, g, t + 1, other)
+        if t == Y // 2 - 1:
+            part = pl.ds(g * (BLOCKS // 2), BLOCKS // 2)
+            src, dst = src.at[part], dst.at[part]
+        return pltpu.make_async_remote_copy(
+            src_ref=src, dst_ref=dst,
             send_sem=y_send.at[g, t, other, kv], recv_sem=y_recv.at[g, t, other, kv],
             device_id=(right, left)[g], device_id_type=MESH,
         )
@@ -184,35 +186,6 @@
             send_sem=w_send.at[0, 0], recv_sem=w_recv.at[xo, o],
             device_id=across, device_id_type=MESH,
         )
-
-    def relay_parts(kv, oy, o):
-        if kv == 0:
-            yield pick_k.at[1, pl.ds(o * 2, 2)], x_send.at[1, o], relay_k.at[pl.ds(o * 2, 2)], o, (
-                got_k.at[pl.ds(o * 2, 2)], x_recv.at[0, o], (seq_of(2, y, z), i))
-        else:
-            for dz in range(2):
-                yield pick_v.at[2 * Z + dz, pl.ds(oy * 2, 2)], w_send.at[2 * Z + dz, oy], relay_v.at[dz, pl.ds(oy * 2, 2)], (
-                    PLANE + dz * Y + oy), (
-                    got_v.at[pl.ds((oy * Z + z) * 2, 2)], w_recv.at[0, oy * Z + z],
-                    (seq_of(2, y, 1 - z if dz else z), twin if dz else i))
-
-    def relay_in(kv, oy, o):
-        return [
-            pltpu.make_async_remote_copy(
-                src_ref=src, dst_ref=buf, send_sem=send, recv_sem=r_recv.at[n],
-                device_id=(seq_of(X - 1, y, z), i), device_id_type=MESH,
-            )
-            for src, send, buf, n, _ in relay_parts(kv, oy, o)
-        ]
-
-    def relay_out(kv, oy, o):
-        return [
-            pltpu.make_async_remote_copy(
-                src_ref=buf, dst_ref=to[0], send_sem=r_send.at[n], recv_sem=to[1],
-                device_id=to[2], device_id_type=MESH,
-            )
-            for _, _, buf, n, to in relay_parts(kv, oy, o)
-        ]
 
     def select(kv, src, oy, o):
         for e in range(2):
@@ -230,29 +203,15 @@
 
     def forward(kv, oy, o):
         for dx in range(X - 1, -1, -1):
-            def direct():
+            @pl.when(x + dx < X)
+            def _():
                 if kv == 1:
                     w_copy(dx, 1, oy).start()
                 if dx > 0:
                     (x_copy(dx, o) if kv == 0 else w_copy(dx, 0, oy)).start()
-            if dx == 2:
-                @pl.when(x == 0)
-                def _():
-                    for copy in relay_in(kv, oy, o):
-                        copy.start()
-                pl.when(x == 1)(direct)
-            else:
-                pl.when(x + dx < X)(direct)
-
-    def relay(kv, oy, o):
-        @pl.when(x == X - 1)
-        def _():
-            for copy in relay_in(kv, oy, o):
-                copy.wait_recv()
-            for copy in relay_out(kv, oy, o):
-                copy.start()
 
     pending = []
+    q_order = [4, 3, 5, 2, 6, 1, 7]
 
     def pick(kv, g, t, other):
         oy = lax.rem(y + (Y - t if g == 0 else t), Y)
@@ -261,8 +220,8 @@
         pending.append((kv, oy, o))
         if len(pending) > 1:
             forward(*pending[-2])
-        if len(pending) > LAG:
-            relay(*pending[-LAG - 1])
+        if len(pending) >= Q_FIRST and (len(pending) - Q_FIRST) % Q_EVERY == 0 and q_order:
+            q_copy(lax.rem(i + q_order.pop(0), GROUP)).start()
 
     for kv in range(2):
         own[kv].wait()
@@ -282,15 +241,15 @@
     for t in range(1, half + 1):
         for kv, other in travels:
             for g in range(2):
-                if t == half and g != (kv + other) % 2:
-                    continue
                 ring_copy(g, t - 1, other, kv).wait_recv()
-                if t < half - 1 or (t == half - 1 and g == (kv + other) % 2):
+                if t < half:
                     ring_copy(g, t, other, kv).start()
-                pick(kv, g, t, other)
+                    pick(kv, g, t, other)
+            if t == half:
+                pick(kv, 0, t, other)
     forward(*pending[-1])
-    for step in pending[-LAG:]:
-        relay(*step)
+    for j in q_order:
+        q_copy(lax.rem(i + j, GROUP)).start()
 
     own[2].wait()
     for j in range(1, GROUP):
@@ -384,8 +343,7 @@
     for t in range(half):
         for kv, other in travels:
             for g in range(2):
-                if t < half - 1 or g == (kv + other) % 2:
-                    ring_copy(g, t, other, kv).wait_send()
+                ring_copy(g, t, other, kv).wait_send()
     for dx in range(X):
         @pl.when(x + dx < X)
         def _():
@@ -397,14 +355,6 @@
                     x_copy(dx, oy * Z + 1).wait_send()
                 return carry
             lax.fori_loop(0, Y, one, 0)
-    @pl.when(x == X - 1)
-    def _():
-        def one(oy, carry):
-            for kv, az in ((0, 0), (0, 1), (1, z)):
-                for copy in relay_out(kv, oy, oy * Z + az):
-                    copy.wait_send()
-            return carry
-        lax.fori_loop(0, Y, one, 0)
     back.wait()
     for j in range(1, GROUP):
         p = lax.rem(i + j, GROUP)
@@ -434,8 +384,6 @@
             [pltpu.VMEM((BLOCKS, BLOCK, WIDTH), bf16)] * Y,
             pltpu.VMEM((X - 1, PLANE * 2, BLOCK, WIDTH), bf16),
             pltpu.VMEM((X * Z, Y * 2, BLOCK, WIDTH), bf16),
-            pltpu.VMEM((PLANE * 2, BLOCK, WIDTH), bf16),
-            pltpu.VMEM((Z, Y * 2, BLOCK, WIDTH), bf16),
             pltpu.VMEM((X * PLANE * 2, BLOCK, WIDTH), bf16),
             pltpu.VMEM((X * PLANE * 2, BLOCK, WIDTH), bf16),
             dma((GROUP,)), dma((GROUP,)), dma((GROUP,)), dma((GROUP,)), dma((GROUP,)), dma((GROUP,)),
@@ -443,7 +391,6 @@
             dma((2, half, 2, 2)), dma((2, half, 2, 2)),
             dma((X - 1, PLANE)), dma((X, PLANE)),
             dma((X * Z, Y)), dma((X, PLANE)),
-            dma((2 * PLANE,)), dma((2 * PLANE,)),
             dma((GROUP, 2)), dma((GROUP, 2)),
             dma((4,)),
         ],

time: 155 us -> 131 us (0.85)
  Pallas kernels: 149 us -> 126 us
    pallas_call x1, Pallas kernels: 149 us -> 126 us  [body(): pl.pallas_call(kernel, out_shape=jax.ShapeDtypeStruct(queries.shape, bf16...]
where the time goes in v3:
time: 131 us
  Pallas kernels  126 us (96%)
  local copies, waits for them, and re-layouts  4.33 us (3%)
    pallas_call x1, Pallas kernels, body(): pl.pallas_call(kernel, out_shape=jax.ShapeDtypeStruct(queries.shape, bf16...  126 us

profile of v3, /device:TPU:6, one launch (start us, length us, event | category | flops | bytes accessed | tf_op | source)
XLA Modules:
  0.0 130.7 jit_solution(3227457559354613897)
XLA Ops:
  0.0 1.0 reshape.15
  1.1 0.1 copy.8
  1.2 0.7 reshape.16.fetch
  1.9 126.4 %shard_map.64 = bf16[128,5120]{1,0:T(8,128)(2,1)} custom-call(s32[256]{0:T(256)} %reshape.16.fetch, s32[16,16]{1,0:T(8,128)} %choose.1, s32[16]{0:T(128)} %live.1, bf16[128,5120]{1,0:T(8,128)(2,1)} %q_in.1, bf16[2,64,1024]{2,1,0:T(8,128)(2,1)} %bitcast.8, bf16[2,64,1024]{2,1,0:T(8,128)(2,1)} %bitcast.9), custom_call_target="tpu_custom_call" | custom-call | tf_op jit(solution)/shard_map/pallas_call | solution.py:375
  128.3 2.5 %copy.10 = bf16[128,5120]{1,0:T(8,128)(2,1)} copy(bf16[128,5120]{1,0:T(8,128)(2,1)} %shard_map.64) | data formatting | bytes 2621440
  (1 shorter events, 0.0 us)

commit v4 on v3

--- a/solution.py
+++ b/solution.py
@@ -21,6 +21,7 @@
 BLOCKS = TOKENS // BLOCK
 QW = REPEAT * WIDTH
 Q_FIRST, Q_EVERY = 3, 2
+PIECES = GROUP // 2
 SCALE = math.log2(math.e) / math.sqrt(WIDTH)
 
 
@@ -39,11 +40,15 @@
     return t if g == 0 or t in (0, Y // 2) else Y // 2 + t
 
 
+def xor2(a, n):
+    return 2 * lax.rem(a // 2 + n // 2, 2) + lax.rem(lax.rem(a, 2) + n % 2, 2)
+
+
 def kernel(
-    fetch, choose, live, q_in, k_in, v_in, o_out,
-    q_all, out_buf, items_k, items_v, pick_k, pick_v, got_k, got_v,
+    fetch_in, choose, live, q_in, k_in, v_in, o_out,
+    fetch, q_all, out_buf, items_k, items_v, pick_k, pick_v, got_k, got_v,
     q_send, q_recv, k_send, k_recv, v_send, v_recv,
-    z_send, z_recv, y_send, y_recv, x_send, x_recv, w_send, w_recv, o_send, o_recv, local_sem,
+    z_send, z_recv, f_send, f_recv, y_send, y_recv, x_send, x_recv, w_send, w_recv, o_send, o_recv, local_sem, f_sem,
 ):
     s = lax.axis_index("seq")
     i = lax.axis_index("head")
@@ -71,12 +76,21 @@
                 barrier, inc=1, device_id=(seq_of(lax.rem(x + j, X), y, az), ai), device_id_type=MESH
             )
 
+    fetches = [
+        pltpu.make_async_copy(fetch_in.at[seq_of(ax, y, az)], fetch.at[ax * Z + az], f_sem.at[ax * Z + az])
+        for ax in range(X) for az in range(Z)
+    ]
+    for copy in fetches:
+        copy.start()
+
     for xo in range(1, X):
         @pl.when(xo > x)
         def _():
             for got in gots:
                 got[pl.ds(xo * PLANE * 2, PLANE * 2)] = jnp.zeros((PLANE * 2, BLOCK, WIDTH), jnp.bfloat16)
 
+    for copy in fetches:
+        copy.wait()
     pl.semaphore_wait(barrier, GROUP - 1 + 3 + 2 * (X - 1))
 
     def rows_of(p):
@@ -146,6 +160,24 @@
             device_id=(right, left)[g], device_id_type=MESH,
         )
 
+    def piece(n):
+        return xor2(i // 2, n)
+
+    def first_copy(g, kv, c):
+        part = pl.ds(4 * c, 4)
+        return pltpu.make_async_remote_copy(
+            src_ref=item(kv, g, 0, 0).at[part], dst_ref=item(kv, g, 1, 0).at[part],
+            send_sem=f_send.at[g, kv, c], recv_sem=f_recv.at[g, kv, c],
+            device_id=(right, left)[g], device_id_type=MESH,
+        )
+
+    def ring_wait(g, t, other, kv):
+        if t == 0 and other == 0:
+            for c in range(PIECES):
+                first_copy(g, kv, c).wait_recv()
+        else:
+            ring_copy(g, t, other, kv).wait_recv()
+
     def z_copy(kv):
         return pltpu.make_async_remote_copy(
             src_ref=item(kv, 0, 0, 0), dst_ref=item(kv, 0, 0, 1), send_sem=z_send.at[kv], recv_sem=z_recv.at[kv],
@@ -153,7 +185,7 @@
         )
 
     def wanted(ax, az, o, e):
-        return fetch[((ax * Z + az) * PLANE + o) * 2 + e]
+        return fetch[ax * Z + az, e, x * PLANE + o]
 
     def x_copy(dx, o):
         return pltpu.make_async_remote_copy(
@@ -225,10 +257,18 @@
 
     for kv in range(2):
         own[kv].wait()
-        for j in range(1, GROUP):
-            head_arrival(kv, lax.rem(i + j, GROUP)).wait_recv()
-        ring_copy(0, 0, 0, kv).start()
-        ring_copy(1, 0, 0, kv).start()
+        for n in range(PIECES):
+            c = piece(n)
+            for core in range(2):
+                p = 2 * c + core
+                if n > 0:
+                    head_arrival(kv, p).wait_recv()
+                else:
+                    @pl.when(p != i)
+                    def _():
+                        head_arrival(kv, p).wait_recv()
+            first_copy(0, kv, c).start()
+            first_copy(1, kv, c).start()
         if kv == 0:
             z_copy(0).start()
         pick(kv, 0, 0, 0)
@@ -237,11 +277,11 @@
     ring_copy(1, 0, 1, 0).start()
     pick(0, 0, 0, 1)
     half = Y // 2
-    travels = ((1, 0), (0, 0), (0, 1))
+    travels = ((0, 0), (1, 0), (0, 1))
     for t in range(1, half + 1):
         for kv, other in travels:
             for g in range(2):
-                ring_copy(g, t - 1, other, kv).wait_recv()
+                ring_wait(g, t - 1, other, kv)
                 if t < half:
                     ring_copy(g, t, other, kv).start()
                     pick(kv, g, t, other)
@@ -343,7 +383,11 @@
     for t in range(half):
         for kv, other in travels:
             for g in range(2):
-                ring_copy(g, t, other, kv).wait_send()
+                if t == 0 and other == 0:
+                    for c in range(PIECES):
+                        first_copy(g, kv, c).wait_send()
+                else:
+                    ring_copy(g, t, other, kv).wait_send()
     for dx in range(X):
         @pl.when(x + dx < X)
         def _():
@@ -363,10 +407,7 @@
 
 
 def body(queries, keys, values, fetch_list, choose, live):
-    s = lax.axis_index("seq")
-    fetch = fetch_list.reshape(X, Y, Z, X, PLANE, 2)
-    fetch = lax.dynamic_index_in_dim(fetch, lax.rem(s // Z, Y), 1, keepdims=False)
-    fetch = lax.dynamic_index_in_dim(fetch, s // PLANE, 2, keepdims=False).reshape(-1)
+    fetch = fetch_list.transpose(0, 2, 1)
     dma = pltpu.SemaphoreType.DMA
     half = Y // 2
     smem = pl.BlockSpec(memory_space=pltpu.SMEM)
@@ -375,9 +416,10 @@
     return pl.pallas_call(
         kernel,
         out_shape=jax.ShapeDtypeStruct(queries.shape, bf16),
-        in_specs=[smem, smem, smem, anywhere, anywhere, anywhere],
+        in_specs=[anywhere, smem, smem, anywhere, anywhere, anywhere],
         out_specs=anywhere,
         scratch_shapes=[
+            pltpu.SMEM((X * Z, 2, X * PLANE), jnp.int32),
             pltpu.VMEM((TOKENS, QW), bf16),
             pltpu.VMEM((TOKENS, QW), bf16),
             [pltpu.VMEM((BLOCKS, BLOCK, WIDTH), bf16)] * PLANE,
@@ -388,11 +430,12 @@
             pltpu.VMEM((X * PLANE * 2, BLOCK, WIDTH), bf16),
             dma((GROUP,)), dma((GROUP,)), dma((GROUP,)), dma((GROUP,)), dma((GROUP,)), dma((GROUP,)),
             dma((1,)), dma((1,)),
+            dma((2, 2, PIECES)), dma((2, 2, PIECES)),
             dma((2, half, 2, 2)), dma((2, half, 2, 2)),
             dma((X - 1, PLANE)), dma((X, PLANE)),
             dma((X * Z, Y)), dma((X, PLANE)),
             dma((GROUP, 2)), dma((GROUP, 2)),
-            dma((4,)),
+            dma((4,)), dma((X * Z,)),
         ],
         compiler_params=pltpu.CompilerParams(
             collective_id=0, has_side_effects=True, vmem_limit_bytes=56 * 1024 * 1024

time: 131 us -> 127 us (0.969)
  local copies, waits for them, and re-layouts: 4.33 us -> 2.46 us
    reshape x2 -> x0, local copies, waits for them, and re-layouts: 1.73 us -> none  [the longest x1 1.03 us: body(): fetch = fetch_list.reshape(X, Y, Z, X, PLANE, 2)]
    pallas_call x1, Pallas kernels: 126 us -> 125 us  [body(): pl.pallas_call(kernel, out_shape=jax.ShapeDtypeStruct(queries.shape, bf16...]
where the time goes in v4:
time: 127 us
  Pallas kernels  125 us (98%)
  local copies, waits for them, and re-layouts  2.46 us (2%)
    pallas_call x1, Pallas kernels, body(): pl.pallas_call(kernel, out_shape=jax.ShapeDtypeStruct(queries.shape, bf16...  125 us

profile of v4, /device:TPU:6, one launch (start us, length us, event | category | flops | bytes accessed | tf_op | source)
XLA Modules:
  0.0 127.2 jit_solution(4256984303689535677)
XLA Ops:
  0.0 124.7 %shard_map.64 = bf16[128,5120]{1,0:T(8,128)(2,1)} custom-call(s32[64,2,64]{2,1,0:T(2,128)} %bitcast.5, s32[16,16]{1,0:T(8,128)} %choose.1, s32[16]{0:T(128)} %live.1, bf16[128,5120]{1,0:T(8,128)(2,1)} %q_in.1, bf16[2,64,1024]{2,1,0:T(8,128)(2,1)} %bitcast.3, bf16[2,64,1024]{2,1,0:T(8,128)(2,1)} %bitcast.4), custom_call_target="tpu_custom_call" | custom-call | tf_op jit(solution)/shard_map/pallas_call | solution.py:416
  124.7 2.5 %copy.8 = bf16[128,5120]{1,0:T(8,128)(2,1)} copy(bf16[128,5120]{1,0:T(8,128)(2,1)} %shard_map.64) | data formatting | bytes 2621440

commit v5 on v4

--- a/solution.py
+++ b/solution.py
@@ -234,7 +234,7 @@
                             pick_v[dx * Z, oy * 2 + e] = src[wanted(x + dx, z, o, e)]
 
     def forward(kv, oy, o):
-        for dx in range(X - 1, -1, -1):
+        for dx in range(X):
             @pl.when(x + dx < X)
             def _():
                 if kv == 1:
@@ -250,8 +250,7 @@
         o = oy * Z + (1 - z if other else z)
         select(kv, item(kv, g, t, other), oy, o)
         pending.append((kv, oy, o))
-        if len(pending) > 1:
-            forward(*pending[-2])
+        forward(*pending[-1])
         if len(pending) >= Q_FIRST and (len(pending) - Q_FIRST) % Q_EVERY == 0 and q_order:
             q_copy(lax.rem(i + q_order.pop(0), GROUP)).start()
 
@@ -287,7 +286,6 @@
                     pick(kv, g, t, other)
             if t == half:
                 pick(kv, 0, t, other)
-    forward(*pending[-1])
     for j in q_order:
         q_copy(lax.rem(i + j, GROUP)).start()
 
@@ -353,17 +351,12 @@
 
     def one_pair(t, carry):
         p = xor3(7 - i, t)
-        attend(p * 2)
-
-        @pl.when(t > 0)
-        def _():
-            out_copy(xor3(7 - i, t - 1), 1).start()
-
-        attend(p * 2 + 1)
-
-        @pl.when(t < GROUP - 1)
-        def _():
-            out_copy(p, 0).start()
+        for half_block in range(2):
+            attend(p * 2 + half_block)
+
+            @pl.when(t < GROUP - 1)
+            def _():
+                out_copy(p, half_block).start()
         return carry
 
     lax.fori_loop(0, GROUP, one_pair, 0)

time: 127 us -> 125 us (0.984)
  Pallas kernels: 125 us -> 122 us
    pallas_call x1, Pallas kernels: 125 us -> 122 us  [body(): pl.pallas_call(kernel, out_shape=jax.ShapeDtypeStruct(queries.shape, bf16...]
where the time goes in v5:
time: 125 us
  Pallas kernels  122 us (98%)
  local copies, waits for them, and re-layouts  2.46 us (2%)
    pallas_call x1, Pallas kernels, body(): pl.pallas_call(kernel, out_shape=jax.ShapeDtypeStruct(queries.shape, bf16...  122 us

profile of v5, /device:TPU:6, one launch (start us, length us, event | category | flops | bytes accessed | tf_op | source)
XLA Modules:
  0.0 124.7 jit_solution(4506997723739275227)
XLA Ops:
  0.0 122.3 %shard_map.64 = bf16[128,5120]{1,0:T(8,128)(2,1)} custom-call(s32[64,2,64]{2,1,0:T(2,128)} %bitcast.5, s32[16,16]{1,0:T(8,128)} %choose.1, s32[16]{0:T(128)} %live.1, bf16[128,5120]{1,0:T(8,128)(2,1)} %q_in.1, bf16[2,64,1024]{2,1,0:T(8,128)(2,1)} %bitcast.3, bf16[2,64,1024]{2,1,0:T(8,128)(2,1)} %bitcast.4), custom_call_target="tpu_custom_call" | custom-call | tf_op jit(solution)/shard_map/pallas_call | solution.py:409
  122.3 2.5 %copy.8 = bf16[128,5120]{1,0:T(8,128)(2,1)} copy(bf16[128,5120]{1,0:T(8,128)(2,1)} %shard_map.64) | data formatting | bytes 2621440

commit v6 on v5

--- a/solution.py
+++ b/solution.py
@@ -271,21 +271,29 @@
         if kv == 0:
             z_copy(0).start()
         pick(kv, 0, 0, 0)
-    z_copy(0).wait_recv()
-    ring_copy(0, 0, 1, 0).start()
-    ring_copy(1, 0, 1, 0).start()
-    pick(0, 0, 0, 1)
     half = Y // 2
     travels = ((0, 0), (1, 0), (0, 1))
-    for t in range(1, half + 1):
-        for kv, other in travels:
-            for g in range(2):
-                ring_wait(g, t - 1, other, kv)
-                if t < half:
-                    ring_copy(g, t, other, kv).start()
-                    pick(kv, g, t, other)
-            if t == half:
-                pick(kv, 0, t, other)
+
+    def ring_step(t, kv, other):
+        for g in range(2):
+            ring_wait(g, t - 1, other, kv)
+            if t < half:
+                ring_copy(g, t, other, kv).start()
+                pick(kv, g, t, other)
+        if t == half:
+            pick(kv, 0, t, other)
+
+    for t in range(1, half + 2):
+        if t <= half:
+            ring_step(t, 0, 0)
+            ring_step(t, 1, 0)
+        if t == 1:
+            z_copy(0).wait_recv()
+            ring_copy(0, 0, 1, 0).start()
+            ring_copy(1, 0, 1, 0).start()
+            pick(0, 0, 0, 1)
+        else:
+            ring_step(t - 1, 0, 1)
     for j in q_order:
         q_copy(lax.rem(i + j, GROUP)).start()
 

time: 125 us -> 121 us (0.968)
  Pallas kernels: 122 us -> 119 us
    pallas_call x1, Pallas kernels: 122 us -> 119 us  [body(): pl.pallas_call(kernel, out_shape=jax.ShapeDtypeStruct(queries.shape, bf16...]
where the time goes in v6:
time: 121 us
  Pallas kernels  119 us (98%)
  local copies, waits for them, and re-layouts  2.46 us (2%)
    pallas_call x1, Pallas kernels, body(): pl.pallas_call(kernel, out_shape=jax.ShapeDtypeStruct(queries.shape, bf16...  119 us
    unnamed x1, local copies, waits for them, and re-layouts  2.46 us

profile of v6, /device:TPU:6, one launch (start us, length us, event | category | flops | bytes accessed | tf_op | source)
XLA Modules:
  0.0 121.2 jit_solution(1523100406648965572)
XLA Ops:
  0.0 118.8 %shard_map.64 = bf16[128,5120]{1,0:T(8,128)(2,1)} custom-call(s32[64,2,64]{2,1,0:T(2,128)} %bitcast.5, s32[16,16]{1,0:T(8,128)} %choose.1, s32[16]{0:T(128)} %live.1, bf16[128,5120]{1,0:T(8,128)(2,1)} %q_in.1, bf16[2,64,1024]{2,1,0:T(8,128)(2,1)} %bitcast.3, bf16[2,64,1024]{2,1,0:T(8,128)(2,1)} %bitcast.4), custom_call_target="tpu_custom_call" | custom-call | tf_op jit(solution)/shard_map/pallas_call | solution.py:417
  118.8 2.5 %copy.8 = bf16[128,5120]{1,0:T(8,128)(2,1)} copy(bf16[128,5120]{1,0:T(8,128)(2,1)} %shard_map.64) | data formatting | bytes 2621440
